TPU v7x, 256 devices: a whole 4x4x8 slice. The times are simulated.
256 devices in a mesh: shift: 4 (over x), fsdp: 32 (over z, y_lo, core), tp: 2 (over y_hi).
Axes of the slice: x: 4, y: 4 (y_hi: 2, y_lo: 2; y = y_hi * 2 + y_lo), z: 8, core: 2. Of those that a mesh axis runs over, the one named last changes fastest.
Arguments:
- grad_stack: float32 [512, 128, 2048], P('shift', 'fsdp', 'tp'), parts along dimension 0, may hold values from -6 to 6
- moment_stack: float32 [512, 128, 2048], P('shift', 'fsdp', 'tp'), parts along dimension 0, may hold values from -6 to 6
- weight_stack: float32 [512, 128, 2048], P('shift', 'fsdp', 'tp'), parts along dimension 0, may hold values from -0.1875 to 0.1875
Outputs:
- new_weights: float32 [512, 128, 2048], P('shift', 'fsdp', 'tp'), parts along dimension 0
- new_momentum: float32 [512, 128, 2048], P('shift', 'fsdp', 'tp'), parts along dimension 0
There are 4 independent parts, one for each index of `shift`. A program takes and returns all parts, laid end to end along the dimension named above; each array names one. Nothing has to cross between parts.
All inputs are finite; a program needn't handle non-finite values.
Results may differ from a plain program's by a relative error of at most 0.0003.
Values sent between devices are 32-bit elements.
No kernel may reach another device: no remote copies, remote signals or barrier semaphores. Data moves between devices by JAX's collectives and lax.ppermute only.
A program may use at most 64 MiB of HBM per device.

v0:
```python
import jax
import jax.numpy as jnp
from jax import lax
from jax.sharding import PartitionSpec as P

ITERS = 3


hold_rate = 0.95
learn_rate = 0.9


def gathered_total(array, axis):
    return lax.all_gather(array, axis).sum(0)


def body(grad_stack, moment_stack, weight_stack):
    new_momentum = hold_rate * moment_stack + grad_stack
    moved = lax.all_to_all(new_momentum, "fsdp", split_axis=0, concat_axis=1, tiled=True)
    total = gathered_total(jnp.sum(moved * moved, axis=(1, 2), keepdims=True), "tp")
    iterate = moved * lax.rsqrt(total + 1e-06)
    for step in range(ITERS):
        gram = gathered_total(
            jnp.einsum("mik,mjk->mij", iterate, iterate, precision=lax.Precision.HIGHEST), "tp"
        )
        mixed = -4.775 * gram + 2.0315 * jnp.einsum(
            "mij,mjk->mik", gram, gram, precision=lax.Precision.HIGHEST
        )
        iterate = 3.4445 * iterate + jnp.einsum(
            "mij,mjk->mik", mixed, iterate, precision=lax.Precision.HIGHEST
        )
    back = lax.all_to_all(iterate, "fsdp", split_axis=1, concat_axis=0, tiled=True)
    new_weights = weight_stack - learn_rate * back
    return (new_weights, new_momentum)


def solution(mesh):
    in_specs = (P("shift", "fsdp", "tp"), P("shift", "fsdp", "tp"), P("shift", "fsdp", "tp"))
    out_specs = (P("shift", "fsdp", "tp"), P("shift", "fsdp", "tp"))
    return jax.shard_map(body, mesh=mesh, in_specs=in_specs, out_specs=out_specs, check_vma=False)
```

profile of v0, /device:TPU:1, one launch (start us, length us, event | category | flops | bytes accessed | tf_op | source)
XLA Modules:
  0.0 186.9 jit_solution(4581866831942809648)
XLA Ops:
  0.6 4.6 %multiply_add_fusion.3 = f32[128,4,1024]{2,1,0:T(4,128)} fusion(f32[128,4,1024]{2,1,0:T(4,128)} %param.3, f32[128,4,1024]{2,1,0:T(4,128)} %param.4), kind=kLoop, calls=%fused_computation.6 | loop fusion | flops 1048576 | bytes 6291456 | tf_op jit(solution)/shard_map/add | solution.py:18
  5.2 11.3 %all-to-all-start = ((f32[128,4,1024]{2,1,0:T(4,128)}), f32[128,4,1024]{2,1,0:T(4,128)S(1)}, u32[]{:S(2)}, u32[]{:S(2)}) async-start(f32[128,4,1024]{2,1,0:T(4,128)} %multiply_add_fusion.3), calls=%async_computation | async-start | bytes 4194304 | tf_op jit(solution)/shard_map/all_to_all | solution.py:19
  16.5 0.6 dynamic-slice
  17.7 48.8 %all-to-all-done = f32[128,4,1024]{2,1,0:T(4,128)S(1)} async-done(((f32[128,4,1024]{2,1,0:T(4,128)}), f32[128,4,1024]{2,1,0:T(4,128)S(1)}, u32[]{:S(2)}, u32[]{:S(2)}) %all-to-all-start) | async-done | bytes 2097184 | tf_op jit(solution)/shard_map/all_to_all | solution.py:19
  66.5 0.6 multiply_reduce_fusion
  67.4 5.3 %all-reduce = f32[8]{0:T(128)S(1)} all-reduce(f32[8]{0:T(128)S(1)} %dynamic-update-slice), channel_id=2, replica_groups=mesh['shift'=4,'fsdp'=32,'tp'=2] {'tp'}, use_global_device_ids=true, to_apply=%add | all-reduce | flops 8 | bytes 64
  72.7 1.5 copy_bitcast_fusion
  74.3 2.0 %all_to_all.23 = f32[4,128,1024]{2,1,0:T(8,128)S(1)} reshape(f32[4,32,4,1024]{3,2,1,0:T(4,128)} %copy_bitcast_fusion) | data formatting | bytes 4194304 | tf_op jit(solution)/shard_map/all_to_all | solution.py:19
  76.3 2.3 %fusion.2 = f32[4,128,128]{2,1,0:T(8,128)S(1)} fusion(f32[4,128,1024]{2,1,0:T(8,128)S(1)} %all_to_all.23, f32[4]{0:T(128)S(1)} %add_rsqrt_fusion), kind=kOutput, calls=%fused_computation.9 | convolution fusion | flops 805830656 | bytes 2359312 | tf_op jit(solution)/shard_map/mik,mjk->mij/dot_general | solution.py:24
  78.5 7.4 %all-gather.1 = f32[8,128,128]{2,1,0:T(8,128)S(1)} all-gather(f32[4,128,128]{2,1,0:T(8,128)S(1)} %fusion.2), channel_id=3, replica_groups=mesh['shift'=4,'fsdp'=32,'tp'=2] {'tp'}, dimensions={0}, use_global_device_ids=true | all-gather | bytes 786432 | tf_op jit(solution)/shard_map/all_gather | solution.py:14
  86.0 0.4 fusion.8
  86.4 4.3 %multiply_add_fusion.2 = f32[4,128,1024]{2,1,0:T(8,128)S(1)} fusion(f32[4,128,1024]{2,1,0:T(8,128)} %copy-done.1, f32[4,128,128]{2,1,0:T(8,128)S(1)} %fusion.8, f32[4]{0:T(128)S(1)} %add_rsqrt_fusion), kind=kOutput, calls=%fused_computation.4 | convolution fusion | flops 807403520 | bytes 4456464 | tf_op jit(solution)/shard_map/mij,mjk->mik/dot_general | solution.py:29
  90.7 2.0 %fusion.11 = f32[4,128,128]{2,1,0:T(8,128)S(1)} fusion(f32[4,128,1024]{2,1,0:T(8,128)S(1)} %multiply_add_fusion.2), kind=kOutput, calls=%fused_computation.21 | convolution fusion | flops 805306368 | bytes 2359296 | tf_op jit(solution)/shard_map/mik,mjk->mij/dot_general | solution.py:24
  92.7 7.6 %all-gather.2 = f32[8,128,128]{2,1,0:T(8,128)S(1)} all-gather(f32[4,128,128]{2,1,0:T(8,128)S(1)} %fusion.11), channel_id=4, replica_groups=mesh['shift'=4,'fsdp'=32,'tp'=2] {'tp'}, dimensions={0}, use_global_device_ids=true | all-gather | bytes 786432 | tf_op jit(solution)/shard_map/all_gather | solution.py:14
  100.3 0.4 fusion.7
  100.7 2.0 %multiply_add_fusion.1 = f32[4,128,1024]{2,1,0:T(8,128)S(1)} fusion(f32[4,128,1024]{2,1,0:T(8,128)S(1)} %multiply_add_fusion.2, f32[4,128,128]{2,1,0:T(8,128)S(1)} %fusion.7), kind=kOutput, calls=%fused_computation.3 | convolution fusion | flops 806354944 | bytes 4456448 | tf_op jit(solution)/shard_map/mij,mjk->mik/dot_general | solution.py:29
  102.8 2.0 %fusion.12 = f32[4,128,128]{2,1,0:T(8,128)S(1)} fusion(f32[4,128,1024]{2,1,0:T(8,128)S(1)} %multiply_add_fusion.1), kind=kOutput, calls=%fused_computation.22 | convolution fusion | flops 805306368 | bytes 2359296 | tf_op jit(solution)/shard_map/mik,mjk->mij/dot_general | solution.py:24
  104.8 7.4 %all-gather.3 = f32[8,128,128]{2,1,0:T(8,128)S(1)} all-gather(f32[4,128,128]{2,1,0:T(8,128)S(1)} %fusion.12), channel_id=5, replica_groups=mesh['shift'=4,'fsdp'=32,'tp'=2] {'tp'}, dimensions={0}, use_global_device_ids=true | all-gather | bytes 786432 | tf_op jit(solution)/shard_map/all_gather | solution.py:14
  112.6 4.2 %multiply_add_fusion = f32[4,128,1024]{2,1,0:T(8,128)S(1)} fusion(f32[4,128,1024]{2,1,0:T(8,128)} %copy-done, f32[4,128,128]{2,1,0:T(8,128)S(1)} %fusion.6), kind=kOutput, calls=%fused_computation.2 | convolution fusion | flops 806354944 | bytes 4456448 | tf_op jit(solution)/shard_map/mij,mjk->mik/dot_general | solution.py:29
  116.9 1.4 copy.8
  118.2 63.8 %all_to_all.27 = f32[4,128,1024]{2,0,1:T(4,128)S(1)} all-to-all(f32[4,128,1024]{2,0,1:T(4,128)S(1)} %copy.8), channel_id=1, replica_groups=mesh['shift'=4,'fsdp'=32,'tp'=2] {'fsdp'}, dimensions={1} | all-to-all | bytes 4194304 | tf_op jit(solution)/shard_map/all_to_all | solution.py:32
  182.0 0.7 broadcast_multiply_fusion
  182.7 1.8 copy.9
  184.5 2.4 %bitcast_subtract_fusion = f32[128,4,1024]{2,1,0:T(4,128)} fusion(f32[128,4,1024]{2,1,0:T(4,128)S(1)} %copy-done.2, f32[32,4,4,1024]{3,2,1,0:T(4,128)S(1)} %copy.9), kind=kLoop, calls=%fused_computation | loop fusion | flops 524288 | bytes 6291456 | tf_op jit(solution)/shard_map/sub | solution.py:33
  (17 shorter events, 0.8 us)
Async XLA Ops:
  5.2 11.3 %copy-start.3 = (u32[256]{0:T(256)S(1)}, u32[256]{0:T(256)}, u32[]{:S(2)}) copy-start(u32[256]{0:T(256)} %constant.19) | copy-start | bytes 3076
  5.2 61.3 %all-to-all-start = ((f32[128,4,1024]{2,1,0:T(4,128)}), f32[128,4,1024]{2,1,0:T(4,128)S(1)}, u32[]{:S(2)}, u32[]{:S(2)}) async-start(f32[128,4,1024]{2,1,0:T(4,128)} %multiply_add_fusion.3), calls=%async_computation | async-start | bytes 4194304 | tf_op jit(solution)/shard_map/all_to_all | solution.py:19
  76.3 9.7 %copy-start.1 = (f32[4,128,1024]{2,1,0:T(8,128)}, f32[4,128,1024]{2,1,0:T(8,128)S(1)}, u32[]{:S(2)}) copy-start(f32[4,128,1024]{2,1,0:T(8,128)S(1)} %all_to_all.23) | copy-start | bytes 6291460
  102.7 2.1 %copy-start = (f32[4,128,1024]{2,1,0:T(8,128)}, f32[4,128,1024]{2,1,0:T(8,128)S(1)}, u32[]{:S(2)}) copy-start(f32[4,128,1024]{2,1,0:T(8,128)S(1)} %multiply_add_fusion.1) | copy-start | bytes 6291460
  182.7 1.8 copy-start.2
where the time goes:
time: 187 us
  blocking collectives  91.4 us (49%)
  waiting for transfers between devices  48.8 us (26%)
  matrix products  18 us (10%)
  starting transfers between devices  11.3 us (6%)
  other arithmetic  8.38 us (4%)
  local copies, waits for them, and re-layouts  7.56 us (4%)
    all_to_all x1, blocking collectives, body(): lax.all_to_all(iterate, 'fsdp', split_axis=1, concat_axis=0, tiled=True)  63.8 us
    all_to_all x1, waiting for transfers between devices, body(): lax.all_to_all(new_momentum, 'fsdp', split_axis=0, concat_axis=1, tiled=T...  48.8 us
    all_gather x3, blocking collectives, gathered_total(): return lax.all_gather(array, axis).sum(0)  22.4 us
    all_to_all x1, starting transfers between devices, body(): lax.all_to_all(new_momentum, 'fsdp', split_axis=0, concat_axis=1, tiled=T...  11.3 us
    dot_general x3, matrix products, body(): jnp.einsum('mij,mjk->mik', mixed, iterate, precision=lax.Precision.HIGHEST)  10.6 us
    dot_general x3, matrix products, body(): jnp.einsum('mik,mjk->mij', iterate, iterate, precision=lax.Precision.HIGH...  6.35 us
    unnamed x1, blocking collectives  5.26 us
    add x1, other arithmetic, body(): new_momentum = hold_rate * moment_stack + grad_stack  4.57 us
  transfers between devices with their start and end apart: 1, of which 1 were waited for; matrix products, arithmetic and copies ran while one was open for 0% of the time, Pallas kernels for 0%

commit v1 on v0

v1 whole, which is shorter than its diff:
```python
import functools

import jax
import jax.numpy as jnp
from jax import lax
from jax.experimental import pallas as pl
from jax.experimental.pallas import tpu as pltpu
from jax.sharding import PartitionSpec as P

ITERS = 3
CHUNKS = 1


hold_rate = 0.95
learn_rate = 0.9

dot = functools.partial(
    lax.dot_general, precision=lax.Precision.HIGHEST, preferred_element_type=jnp.float32
)
ROW_BY_ROW = (((1,), (1,)), ((), ()))
PLAIN = (((1,), (0,)), ((), ()))


def step_matrix(gram):
    side = gram.shape[0]
    row = lax.broadcasted_iota(jnp.int32, (side, side), 0)
    col = lax.broadcasted_iota(jnp.int32, (side, side), 1)
    diagonal = row == col
    total = jnp.sum(jnp.where(diagonal, gram, 0.0))
    inverse = lax.rsqrt(total + 1e-06)
    gram = (gram * inverse) * inverse
    product = None
    for step in range(ITERS):
        square = dot(gram, gram, PLAIN)
        factor = jnp.where(diagonal, 3.4445, 0.0) + (-4.775 * gram + 2.0315 * square)
        if step < ITERS - 1:
            gram = dot(dot(factor, gram, PLAIN), factor, PLAIN)
        product = factor if product is None else dot(factor, product, PLAIN)
    return product * (learn_rate * inverse)


def matrix_kernel(moved_ref, out_ref, whole_ref):
    rows, halves, few, wide = moved_ref.shape[1:]
    for row in range(rows):
        for half in range(halves):
            whole_ref[row * few : (row + 1) * few, half * wide : (half + 1) * wide] = moved_ref[0, row, half]
    whole = whole_ref[...]
    gram = dot(whole, whole, ROW_BY_ROW)
    whole_ref[...] = dot(step_matrix(gram), whole, PLAIN)
    for row in range(rows):
        for half in range(halves):
            out_ref[0, row, half] = whole_ref[row * few : (row + 1) * few, half * wide : (half + 1) * wide]


def update_matrices(moved):
    mats, rows, halves, few, wide = moved.shape
    side, width = rows * few, halves * wide
    flops = mats * (6 * 2) * (2 * side * side * width + 9 * side**3)
    block = pl.BlockSpec((1, rows, halves, few, wide), lambda m: (m, 0, 0, 0, 0))
    return pl.pallas_call(
        matrix_kernel,
        grid=(mats,),
        out_shape=jax.ShapeDtypeStruct(moved.shape, jnp.float32),
        in_specs=[block],
        out_specs=block,
        scratch_shapes=[pltpu.VMEM((side, width), jnp.float32)],
        cost_estimate=pl.CostEstimate(flops=flops, bytes_accessed=2 * 4 * moved.size, transcendentals=0),
    )(moved)


def body(grad_stack, moment_stack, weight_stack):
    mats, few, wide = grad_stack.shape
    rows, halves = lax.axis_size("fsdp"), lax.axis_size("tp")
    group = rows * halves
    own = mats // CHUNKS // group
    new_momentum = hold_rate * moment_stack + grad_stack
    pieces = []
    for chunk in jnp.split(new_momentum, CHUNKS):
        sent = chunk.reshape(group, own, few, wide)
        moved = lax.all_to_all(sent, ("fsdp", "tp"), split_axis=0, concat_axis=0, tiled=True)
        moved = moved.reshape(rows, halves, own, few, wide).transpose(2, 0, 1, 3, 4)
        change = update_matrices(moved).transpose(1, 2, 0, 3, 4).reshape(group, own, few, wide)
        back = lax.all_to_all(change, ("fsdp", "tp"), split_axis=0, concat_axis=0, tiled=True)
        pieces.append(back.reshape(mats // CHUNKS, few, wide))
    new_weights = weight_stack - jnp.concatenate(pieces)
    return (new_weights, new_momentum)


def solution(mesh):
    in_specs = (P("shift", "fsdp", "tp"), P("shift", "fsdp", "tp"), P("shift", "fsdp", "tp"))
    out_specs = (P("shift", "fsdp", "tp"), P("shift", "fsdp", "tp"))
    return jax.shard_map(body, mesh=mesh, in_specs=in_specs, out_specs=out_specs, check_vma=False)
```

time: 187 us -> 144 us (0.77)
  waiting for transfers between devices: 48.8 us -> 0 us
  blocking collectives: 91.4 us -> 122 us
  matrix products: 18 us -> 0 us
  Pallas kernels: 0 us -> 12.5 us
  starting transfers between devices: 11.3 us -> 0 us
  local copies, waits for them, and re-layouts: 7.56 us -> 3.26 us
  other arithmetic: 8.38 us -> 5.63 us
    all_to_all x1 -> x2, blocking collectives: 63.8 us -> 122 us  [the longest x1 64.3 us: body(): lax.all_to_all(sent, ('fsdp', 'tp'), split_axis=0, concat_axis=0, tiled=T...]
    all_to_all x1 -> x0, waiting for transfers between devices: 48.8 us -> none  [body(): lax.all_to_all(new_momentum, 'fsdp', split_axis=0, concat_axis=1, tiled=T...]
    all_gather x3 -> x0, blocking collectives: 22.4 us -> none  [gathered_total(): return lax.all_gather(array, axis).sum(0)]
    dot_general x9 -> x0, matrix products: 18 us -> none  [the longest x3 10.6 us: body(): jnp.einsum('mij,mjk->mik', mixed, iterate, precision=lax.Precision.HIGHEST)]
    pallas_call x0 -> x1, Pallas kernels: none -> 12.5 us  [update_matrices(): pl.pallas_call(matrix_kernel, grid=(mats,), out_shape=jax.ShapeDtypeStruc...]
    all_to_all x1 -> x0, starting transfers between devices: 11.3 us -> none  [body(): lax.all_to_all(new_momentum, 'fsdp', split_axis=0, concat_axis=1, tiled=T...]
    unnamed x1 -> x0, blocking collectives: 5.26 us -> none
    all_to_all x2 -> x1, local copies, waits for them, and re-layouts: 3.52 us -> 1.49 us  [body(): lax.all_to_all(sent, ('fsdp', 'tp'), split_axis=0, concat_axis=0, tiled=T...]
  transfers between devices with their start and end apart: 1 -> 0, of which waited for: 1 -> 0; matrix products, arithmetic and copies ran while one was open for 0% -> 0% of each run, Pallas kernels for 0% -> 0%
where the time goes in v1:
time: 144 us
  blocking collectives  122 us (85%)
  Pallas kernels  12.5 us (9%)
  other arithmetic  5.63 us (4%)
  local copies, waits for them, and re-layouts  3.26 us (2%)
    all_to_all x1, blocking collectives, body(): lax.all_to_all(sent, ('fsdp', 'tp'), split_axis=0, concat_axis=0, tiled=T...  64.3 us
    all_to_all x1, blocking collectives, body(): lax.all_to_all(change, ('fsdp', 'tp'), split_axis=0, concat_axis=0, tiled...  57.9 us
    pallas_call x1, Pallas kernels, update_matrices(): pl.pallas_call(matrix_kernel, grid=(mats,), out_shape=jax.ShapeDtypeStruc...  12.5 us
    add x1, other arithmetic, body(): new_momentum = hold_rate * moment_stack + grad_stack  3.25 us

profile of v1, /device:TPU:1, one launch (start us, length us, event | category | flops | bytes accessed | tf_op | source)
XLA Modules:
  0.0 144.2 jit_solution(2153076271105923063)
XLA Ops:
  0.6 3.2 %multiply_add_fusion = f32[128,4,1024]{2,1,0:T(4,128)S(1)} fusion(f32[128,4,1024]{2,1,0:T(4,128)} %param.3, f32[128,4,1024]{2,1,0:T(4,128)} %param.4), kind=kLoop, calls=%fused_computation.1 | loop fusion | flops 1048576 | bytes 6291456 | tf_op jit(solution)/shard_map/add | solution.py:76
  3.9 0.0 copy-start
  3.9 64.3 %all_to_all.10 = f32[64,2,4,1024]{3,2,1,0:T(4,128)S(1)} all-to-all(f32[64,2,4,1024]{3,2,1,0:T(4,128)S(1)} %bitcast.9), channel_id=1, replica_groups=mesh['shift'=4,'fsdp'=32,'tp'=2] {'fsdp','tp'}, dimensions={0} | all-to-all | bytes 4194304 | tf_op jit(solution)/shard_map/all_to_all | solution.py:80
  68.2 0.0 copy-done
  68.2 1.5 %copy.7 = f32[64,2,4,1024]{3,2,0,1:T(4,128)} copy(f32[64,2,4,1024]{3,2,1,0:T(4,128)S(1)} %all_to_all.10) | data formatting | bytes 4194304 | tf_op jit(solution)/shard_map/all_to_all | solution.py:80
  69.7 12.5 %shard_map.50 = f32[2,32,2,4,1024]{4,3,2,1,0:T(4,128)} custom-call(f32[2,32,2,4,1024]{4,3,2,1,0:T(4,128)} %bitcast.10), custom_call_target="tpu_custom_call" | custom-call | flops 2063597568 | bytes 4194304 | tf_op jit(solution)/shard_map/pallas_call | solution.py:60
  82.1 1.8 %copy.8 = f32[64,2,4,1024]{3,2,1,0:T(4,128)S(1)} copy(f32[64,2,4,1024]{3,2,0,1:T(4,128)} %bitcast.11) | data formatting | bytes 4194304 | tf_op jit(solution)/shard_map/reshape | solution.py:82
  83.9 0.0 copy-start.1
  83.9 57.9 %all_to_all.11 = f32[64,2,4,1024]{3,2,1,0:T(4,128)S(1)} all-to-all(f32[64,2,4,1024]{3,2,1,0:T(4,128)S(1)} %copy.8), channel_id=1, replica_groups=mesh['shift'=4,'fsdp'=32,'tp'=2] {'fsdp','tp'}, dimensions={0} | all-to-all | bytes 4194304 | tf_op jit(solution)/shard_map/all_to_all | solution.py:83
  141.8 0.0 copy-done.1
  141.8 2.4 %bitcast_subtract_fusion = f32[128,4,1024]{2,1,0:T(4,128)} fusion(f32[128,4,1024]{2,1,0:T(4,128)S(1)} %copy-done.1, f32[64,2,4,1024]{3,2,1,0:T(4,128)S(1)} %all_to_all.11), kind=kLoop, calls=%fused_computation | loop fusion | flops 524288 | bytes 6291456 | tf_op jit(solution)/shard_map/sub | solution.py:85
Async XLA Ops:
  3.9 64.3 %copy-start = (f32[128,4,1024]{2,1,0:T(4,128)}, f32[128,4,1024]{2,1,0:T(4,128)S(1)}, u32[]{:S(2)}) copy-start(f32[128,4,1024]{2,1,0:T(4,128)S(1)} %multiply_add_fusion) | copy-start | bytes 6291460
  83.9 57.9 %copy-start.1 = (f32[128,4,1024]{2,1,0:T(4,128)S(1)}, f32[128,4,1024]{2,1,0:T(4,128)}, u32[]{:S(2)}) copy-start(f32[128,4,1024]{2,1,0:T(4,128)} %param.5) | copy-start | bytes 6291460

commit v2 on v0

v2 whole, which is shorter than its diff:
```python
import functools

import jax
import jax.numpy as jnp
from jax import lax
from jax.experimental import pallas as pl
from jax.experimental.pallas import tpu as pltpu
from jax.sharding import PartitionSpec as P

ITERS = 3


hold_rate = 0.95
learn_rate = 0.9

ROW_BY_ROW = (((1,), (1,)), ((), ()))
PLAIN = (((1,), (0,)), ((), ()))
dot = functools.partial(lax.dot_general, preferred_element_type=jnp.float32)


def parts_of(value):
    high = value.astype(jnp.bfloat16)
    rest = value - high.astype(jnp.float32)
    middle = rest.astype(jnp.bfloat16)
    low = (rest - middle.astype(jnp.float32)).astype(jnp.bfloat16)
    return high, middle, low


def left_parts(value):
    high, middle, low = parts_of(value)
    return (
        jnp.concatenate([high, high], axis=1),
        jnp.concatenate([middle, middle], axis=1),
        jnp.concatenate([high, low], axis=1),
    )


def right_parts(value):
    high, middle, low = parts_of(value)
    return (
        jnp.concatenate([high, middle], axis=0),
        jnp.concatenate([low, high], axis=0),
    )


def product_of(left, right):
    return (
        dot(left[2], right[1], PLAIN) + dot(left[1], right[0], PLAIN)
    ) + dot(left[0], right[0], PLAIN)


def gram_of(high, middle, low):
    side = high.shape[0]
    first = dot(high, jnp.concatenate([high, middle], axis=0), ROW_BY_ROW)
    small = dot(high, low, ROW_BY_ROW) + first[:, side:]
    return (dot(middle, middle, ROW_BY_ROW) + (small + small.T)) + first[:, :side]


def step_matrices(grams):
    side = grams[0].shape[0]
    row = lax.broadcasted_iota(jnp.int32, (side, side), 0)
    col = lax.broadcasted_iota(jnp.int32, (side, side), 1)
    diagonal = row == col
    inverses = [
        lax.rsqrt(jnp.sum(jnp.where(diagonal, gram, 0.0), axis=(0, 1), keepdims=True) + 1e-06)
        for gram in grams
    ]
    grams = [(gram * inverse) * inverse for gram, inverse in zip(grams, inverses)]
    products = None
    for step in range(ITERS):
        rights = [right_parts(gram) for gram in grams]
        squares = [product_of(left_parts(gram), right) for gram, right in zip(grams, rights)]
        factors = [
            jnp.where(diagonal, 3.4445, 0.0) + (-4.775 * gram + 2.0315 * square)
            for gram, square in zip(grams, squares)
        ]
        lefts = [left_parts(factor) for factor in factors]
        if step < ITERS - 1:
            inner = [product_of(left, right) for left, right in zip(lefts, rights)]
            grams = [product_of(left, right_parts(one)) for left, one in zip(lefts, inner)]
        if products is None:
            products = factors
        else:
            products = [product_of(left, right_parts(one)) for left, one in zip(lefts, products)]
    return [one * (learn_rate * inverse) for one, inverse in zip(products, inverses)]


def matrices_kernel(halves, moved_ref, out_ref, whole_ref):
    senders, own, few, wide = moved_ref.shape
    parts = []
    for mat in range(own):
        for sender in range(senders):
            row, half = divmod(sender, halves)
            whole_ref[mat, row * few : (row + 1) * few, half * wide : (half + 1) * wide] = moved_ref[sender, mat]
        parts.append(parts_of(whole_ref[mat]))
    steps = step_matrices([gram_of(*one) for one in parts])
    for mat, (step, (high, middle, low)) in enumerate(zip(steps, parts)):
        right = (jnp.concatenate([high, middle], axis=0), jnp.concatenate([low, high], axis=0))
        whole_ref[mat] = product_of(left_parts(step), right)
        for sender in range(senders):
            row, half = divmod(sender, halves)
            out_ref[sender, mat] = whole_ref[mat, row * few : (row + 1) * few, half * wide : (half + 1) * wide]


def update_matrices(moved, rows, halves):
    _, own, few, wide = moved.shape
    side, width = rows * few, halves * wide
    flops = own * (6 * 2) * (2 * side * side * width + 9 * side**3)
    return pl.pallas_call(
        functools.partial(matrices_kernel, halves),
        out_shape=jax.ShapeDtypeStruct(moved.shape, jnp.float32),
        in_specs=[pl.BlockSpec(memory_space=pltpu.VMEM)],
        out_specs=pl.BlockSpec(memory_space=pltpu.VMEM),
        scratch_shapes=[pltpu.VMEM((own, side, width), jnp.float32)],
        compiler_params=pltpu.CompilerParams(vmem_limit_bytes=24 << 20),
        cost_estimate=pl.CostEstimate(flops=flops, bytes_accessed=2 * 4 * moved.size, transcendentals=0),
    )(moved)


def body(grad_stack, moment_stack, weight_stack):
    mats, few, wide = grad_stack.shape
    rows, halves = lax.axis_size("fsdp"), lax.axis_size("tp")
    group = rows * halves
    new_momentum = hold_rate * moment_stack + grad_stack
    moved = lax.all_to_all(new_momentum, ("fsdp", "tp"), split_axis=0, concat_axis=0, tiled=True)
    change = update_matrices(moved.reshape(group, mats // group, few, wide), rows, halves)
    back = lax.all_to_all(change.reshape(mats, few, wide), ("fsdp", "tp"), split_axis=0, concat_axis=0, tiled=True)
    new_weights = weight_stack - back
    return (new_weights, new_momentum)


def solution(mesh):
    in_specs = (P("shift", "fsdp", "tp"), P("shift", "fsdp", "tp"), P("shift", "fsdp", "tp"))
    out_specs = (P("shift", "fsdp", "tp"), P("shift", "fsdp", "tp"))
    return jax.shard_map(body, mesh=mesh, in_specs=in_specs, out_specs=out_specs, check_vma=False)
```

time: 187 us -> 133 us (0.71)
  waiting for transfers between devices: 48.8 us -> 0 us
  blocking collectives: 91.4 us -> 122 us
  matrix products: 18 us -> 0 us
  starting transfers between devices: 11.3 us -> 0 us
  local copies, waits for them, and re-layouts: 7.56 us -> 0.01 us
  Pallas kernels: 0 us -> 4.22 us
  other arithmetic: 8.38 us -> 5.5 us
    all_to_all x1 -> x2, blocking collectives: 63.8 us -> 122 us  [the longest x1 64.3 us: body(): lax.all_to_all(new_momentum, ('fsdp', 'tp'), split_axis=0, concat_axis=0,...]
    all_to_all x1 -> x0, waiting for transfers between devices: 48.8 us -> none  [body(): lax.all_to_all(new_momentum, 'fsdp', split_axis=0, concat_axis=1, tiled=T...]
    all_gather x3 -> x0, blocking collectives: 22.4 us -> none  [gathered_total(): return lax.all_gather(array, axis).sum(0)]
    dot_general x9 -> x0, matrix products: 18 us -> none  [the longest x3 10.6 us: body(): jnp.einsum('mij,mjk->mik', mixed, iterate, precision=lax.Precision.HIGHEST)]
    all_to_all x1 -> x0, starting transfers between devices: 11.3 us -> none  [body(): lax.all_to_all(new_momentum, 'fsdp', split_axis=0, concat_axis=1, tiled=T...]
    unnamed x1 -> x0, blocking collectives: 5.26 us -> none
    pallas_call x0 -> x1, Pallas kernels: none -> 4.22 us  [update_matrices(): pl.pallas_call(functools.partial(matrices_kernel, halves), out_shape=jax....]
    all_to_all x2 -> x0, local copies, waits for them, and re-layouts: 3.52 us -> none  [body(): lax.all_to_all(new_momentum, 'fsdp', split_axis=0, concat_axis=1, tiled=T...]
  transfers between devices with their start and end apart: 1 -> 0, of which waited for: 1 -> 0; matrix products, arithmetic and copies ran while one was open for 0% -> 0% of each run, Pallas kernels for 0% -> 0%
where the time goes in v2:
time: 133 us
  blocking collectives  122 us (92%)
  other arithmetic  5.5 us (4%)
  Pallas kernels  4.22 us (3%)
    all_to_all x1, blocking collectives, body(): lax.all_to_all(new_momentum, ('fsdp', 'tp'), split_axis=0, concat_axis=0,...  64.3 us
    all_to_all x1, blocking collectives, body(): lax.all_to_all(change.reshape(mats, few, wide), ('fsdp', 'tp'), split_axi...  57.9 us
    pallas_call x1, Pallas kernels, update_matrices(): pl.pallas_call(functools.partial(matrices_kernel, halves), out_shape=jax....  4.22 us
    add x1, other arithmetic, body(): new_momentum = hold_rate * moment_stack + grad_stack  3.25 us

profile of v2, /device:TPU:1, one launch (start us, length us, event | category | flops | bytes accessed | tf_op | source)
XLA Modules:
  0.0 132.5 jit_solution(5766350008310729131)
XLA Ops:
  0.6 3.2 %multiply_add_fusion = f32[128,4,1024]{2,1,0:T(4,128)S(1)} fusion(f32[128,4,1024]{2,1,0:T(4,128)} %param.3, f32[128,4,1024]{2,1,0:T(4,128)} %param.4), kind=kLoop, calls=%fused_computation | loop fusion | flops 1048576 | bytes 6291456 | tf_op jit(solution)/shard_map/add | solution.py:124
  3.9 0.0 copy-start
  3.9 64.3 %all_to_all.10 = f32[128,4,1024]{2,1,0:T(4,128)S(1)} all-to-all(f32[128,4,1024]{2,1,0:T(4,128)S(1)} %multiply_add_fusion), channel_id=1, replica_groups=mesh['shift'=4,'fsdp'=32,'tp'=2] {'fsdp','tp'}, dimensions={0} | all-to-all | bytes 4194304 | tf_op jit(solution)/shard_map/all_to_all | solution.py:125
  68.2 0.0 copy-done
  68.2 4.2 %shard_map.50 = f32[64,2,4,1024]{3,2,1,0:T(4,128)S(1)} custom-call(f32[64,2,4,1024]{3,2,1,0:T(4,128)S(1)} %bitcast.3), custom_call_target="tpu_custom_call" | custom-call | flops 2063597568 | bytes 4194304 | tf_op jit(solution)/shard_map/pallas_call | solution.py:109
  72.4 0.0 copy-start.1
  72.4 57.9 %all_to_all.11 = f32[128,4,1024]{2,1,0:T(4,128)S(1)} all-to-all(f32[128,4,1024]{2,1,0:T(4,128)S(1)} %bitcast.2), channel_id=1, replica_groups=mesh['shift'=4,'fsdp'=32,'tp'=2] {'fsdp','tp'}, dimensions={0} | all-to-all | bytes 4194304 | tf_op jit(solution)/shard_map/all_to_all | solution.py:127
  130.3 0.0 copy-done.1
  130.3 2.2 %sub.3 = f32[128,4,1024]{2,1,0:T(4,128)} subtract(f32[128,4,1024]{2,1,0:T(4,128)S(1)} %copy-done.1, f32[128,4,1024]{2,1,0:T(4,128)S(1)} %all_to_all.11) | non-fusion elementwise | flops 524288 | bytes 6291456 | tf_op jit(solution)/shard_map/sub | solution.py:128
Async XLA Ops:
  3.9 64.3 %copy-start = (f32[128,4,1024]{2,1,0:T(4,128)}, f32[128,4,1024]{2,1,0:T(4,128)S(1)}, u32[]{:S(2)}) copy-start(f32[128,4,1024]{2,1,0:T(4,128)S(1)} %multiply_add_fusion) | copy-start | bytes 6291460
  72.4 57.9 %copy-start.1 = (f32[128,4,1024]{2,1,0:T(4,128)S(1)}, f32[128,4,1024]{2,1,0:T(4,128)}, u32[]{:S(2)}) copy-start(f32[128,4,1024]{2,1,0:T(4,128)} %param.5) | copy-start | bytes 6291460

commit v3 on v2

--- a/solution.py
+++ b/solution.py
@@ -8,6 +8,9 @@
 from jax.sharding import PartitionSpec as P
 
 ITERS = 3
+MOMENTUM_PIECES = 8
+WEIGHT_PIECES = 8
+GROUP = ("far", "core", "near", "tp")
 
 
 hold_rate = 0.95
@@ -85,8 +88,10 @@
     return [one * (learn_rate * inverse) for one, inverse in zip(products, inverses)]
 
 
-def matrices_kernel(halves, moved_ref, out_ref, whole_ref):
+def matrices_kernel(halves, moved_ref, sent_ref, out_ref, kept_ref, whole_ref, sem):
     senders, own, few, wide = moved_ref.shape
+    keep = pltpu.make_async_copy(sent_ref, kept_ref, sem)
+    keep.start()
     parts = []
     for mat in range(own):
         for sender in range(senders):
@@ -96,40 +101,111 @@
     steps = step_matrices([gram_of(*one) for one in parts])
     for mat, (step, (high, middle, low)) in enumerate(zip(steps, parts)):
         right = (jnp.concatenate([high, middle], axis=0), jnp.concatenate([low, high], axis=0))
-        whole_ref[mat] = product_of(left_parts(step), right)
+        change = product_of(left_parts(step), right)
         for sender in range(senders):
             row, half = divmod(sender, halves)
-            out_ref[sender, mat] = whole_ref[mat, row * few : (row + 1) * few, half * wide : (half + 1) * wide]
-
-
-def update_matrices(moved, rows, halves):
+            out_ref[sender, mat] = change[row * few : (row + 1) * few, half * wide : (half + 1) * wide]
+    keep.wait()
+
+
+def update_matrices(moved, sent, rows, halves):
     _, own, few, wide = moved.shape
     side, width = rows * few, halves * wide
     flops = own * (6 * 2) * (2 * side * side * width + 9 * side**3)
     return pl.pallas_call(
         functools.partial(matrices_kernel, halves),
-        out_shape=jax.ShapeDtypeStruct(moved.shape, jnp.float32),
-        in_specs=[pl.BlockSpec(memory_space=pltpu.VMEM)],
-        out_specs=pl.BlockSpec(memory_space=pltpu.VMEM),
-        scratch_shapes=[pltpu.VMEM((own, side, width), jnp.float32)],
+        out_shape=[jax.ShapeDtypeStruct(moved.shape, jnp.float32), jax.ShapeDtypeStruct(sent.shape, jnp.float32)],
+        in_specs=[pl.BlockSpec(memory_space=pltpu.VMEM)] * 2,
+        out_specs=[pl.BlockSpec(memory_space=pltpu.VMEM), pl.BlockSpec(memory_space=pl.ANY)],
+        scratch_shapes=[pltpu.VMEM((own, side, width), jnp.float32), pltpu.SemaphoreType.DMA],
         compiler_params=pltpu.CompilerParams(vmem_limit_bytes=24 << 20),
         cost_estimate=pl.CostEstimate(flops=flops, bytes_accessed=2 * 4 * moved.size, transcendentals=0),
-    )(moved)
+    )(moved, sent)
+
+
+def momentum_kernel(grad_ref, moment_ref, out_ref, grads, moments, sems):
+    pieces, span = grads.shape[:2]
+    copies = []
+    for piece in range(pieces):
+        mine = pl.ds(piece * span, span)
+        pair = (
+            pltpu.make_async_copy(moment_ref.at[mine], moments.at[piece], sems.at[piece, 0]),
+            pltpu.make_async_copy(grad_ref.at[mine], grads.at[piece], sems.at[piece, 1]),
+        )
+        for copy in pair:
+            copy.start()
+        copies.append(pair)
+    for piece, pair in enumerate(copies):
+        for copy in pair:
+            copy.wait()
+        out_ref[piece * span : (piece + 1) * span] = hold_rate * moments[piece] + grads[piece]
+
+
+def momentum_of(grad, moment):
+    mats, few, wide = grad.shape
+    pieces = (MOMENTUM_PIECES, mats // MOMENTUM_PIECES, few, wide)
+    anywhere = pl.BlockSpec(memory_space=pl.ANY)
+    return pl.pallas_call(
+        momentum_kernel,
+        out_shape=jax.ShapeDtypeStruct(grad.shape, jnp.float32),
+        in_specs=[anywhere, anywhere],
+        out_specs=pl.BlockSpec(memory_space=pltpu.VMEM),
+        scratch_shapes=[
+            pltpu.VMEM(pieces, jnp.float32),
+            pltpu.VMEM(pieces, jnp.float32),
+            pltpu.SemaphoreType.DMA((MOMENTUM_PIECES, 2)),
+        ],
+        compiler_params=pltpu.CompilerParams(vmem_limit_bytes=16 << 20),
+        cost_estimate=pl.CostEstimate(flops=2 * grad.size, bytes_accessed=2 * 4 * grad.size, transcendentals=0),
+    )(
+        pltpu.with_memory_space_constraint(grad, pltpu.HBM),
+        pltpu.with_memory_space_constraint(moment, pltpu.HBM),
+    )
+
+
+def weights_kernel(weight_ref, back_ref, out_ref, news, sems):
+    pieces, span = news.shape[:2]
+    copies = []
+    for piece in range(pieces):
+        mine = slice(piece * span, (piece + 1) * span)
+        news[piece] = weight_ref[mine] - back_ref[mine]
+        copy = pltpu.make_async_copy(news.at[piece], out_ref.at[pl.ds(piece * span, span)], sems.at[piece])
+        copy.start()
+        copies.append(copy)
+    for copy in copies:
+        copy.wait()
+
+
+def weights_of(weight, back):
+    mats, few, wide = weight.shape
+    whole = pl.BlockSpec(memory_space=pltpu.VMEM)
+    return pl.pallas_call(
+        weights_kernel,
+        out_shape=jax.ShapeDtypeStruct(weight.shape, jnp.float32),
+        in_specs=[whole, whole],
+        out_specs=pl.BlockSpec(memory_space=pl.ANY),
+        scratch_shapes=[
+            pltpu.VMEM((WEIGHT_PIECES, mats // WEIGHT_PIECES, few, wide), jnp.float32),
+            pltpu.SemaphoreType.DMA((WEIGHT_PIECES,)),
+        ],
+        compiler_params=pltpu.CompilerParams(vmem_limit_bytes=16 << 20),
+        cost_estimate=pl.CostEstimate(flops=weight.size, bytes_accessed=4 * weight.size, transcendentals=0),
+    )(weight, back)
 
 
 def body(grad_stack, moment_stack, weight_stack):
     mats, few, wide = grad_stack.shape
-    rows, halves = lax.axis_size("fsdp"), lax.axis_size("tp")
-    group = rows * halves
-    new_momentum = hold_rate * moment_stack + grad_stack
-    moved = lax.all_to_all(new_momentum, ("fsdp", "tp"), split_axis=0, concat_axis=0, tiled=True)
-    change = update_matrices(moved.reshape(group, mats // group, few, wide), rows, halves)
-    back = lax.all_to_all(change.reshape(mats, few, wide), ("fsdp", "tp"), split_axis=0, concat_axis=0, tiled=True)
-    new_weights = weight_stack - back
-    return (new_weights, new_momentum)
+    group, halves = lax.axis_size(GROUP), lax.axis_size(GROUP[-1])
+    sent = momentum_of(grad_stack, moment_stack)
+    moved = lax.all_to_all(sent, GROUP, split_axis=0, concat_axis=0, tiled=True)
+    moved = moved.reshape(group, mats // group, few, wide)
+    change, new_momentum = update_matrices(moved, sent, group // halves, halves)
+    back = lax.all_to_all(change.reshape(mats, few, wide), GROUP, split_axis=0, concat_axis=0, tiled=True)
+    return (weights_of(weight_stack, back), new_momentum)
 
 
 def solution(mesh):
-    in_specs = (P("shift", "fsdp", "tp"), P("shift", "fsdp", "tp"), P("shift", "fsdp", "tp"))
-    out_specs = (P("shift", "fsdp", "tp"), P("shift", "fsdp", "tp"))
-    return jax.shard_map(body, mesh=mesh, in_specs=in_specs, out_specs=out_specs, check_vma=False)
+    shift, fsdp, tp = mesh.devices.shape
+    fine = jax.sharding.Mesh(mesh.devices.reshape(shift, fsdp // 4, 2, 2, tp), ("shift", "far", "near", "core", "tp"))
+    spec = P("shift", ("far", "near", "core"), "tp")
+    return jax.shard_map(body, mesh=fine, in_specs=(spec,) * 3, out_specs=(spec,) * 2, check_vma=False)

time: 133 us -> 130 us (0.977)
  other arithmetic: 5.5 us -> 0 us
  Pallas kernels: 4.22 us -> 7.76 us
    pallas_call x1 -> x3, Pallas kernels: 4.22 us -> 7.76 us  [the longest x1 4.05 us: update_matrices(): pl.pallas_call(functools.partial(matrices_kernel, halves), out_shape=[jax...]
    add x1 -> x0, other arithmetic: 3.25 us -> none  [body(): new_momentum = hold_rate * moment_stack + grad_stack]
    sub x1 -> x0, other arithmetic: 2.25 us -> none  [body(): new_weights = weight_stack - back]
where the time goes in v3:
time: 130 us
  blocking collectives  121 us (93%)
  Pallas kernels  7.76 us (6%)
    all_to_all x1, blocking collectives, body(): moved = lax.all_to_all(sent, GROUP, split_axis=0, concat_axis=0, tiled=True)  64.3 us
    all_to_all x1, blocking collectives, body(): lax.all_to_all(change.reshape(mats, few, wide), GROUP, split_axis=0, conc...  57 us
    pallas_call x1, Pallas kernels, update_matrices(): pl.pallas_call(functools.partial(matrices_kernel, halves), out_shape=[jax...  4.05 us

profile of v3, /device:TPU:1, one launch (start us, length us, event | category | flops | bytes accessed | tf_op | source)
XLA Modules:
  0.0 129.7 jit_solution(3434074184169103872)
XLA Ops:
  0.6 2.3 %shard_map.50.sent_ref = f32[128,4,1024]{2,1,0:T(4,128)S(1)} custom-call(f32[128,4,1024]{2,1,0:T(4,128)} %grad_ref.1, f32[128,4,1024]{2,1,0:T(4,128)} %moment_ref.1), custom_call_target="tpu_custom_call" | custom-call | flops 1048576 | bytes 4194304 | tf_op jit(solution)/shard_map/pallas_call | solution.py:148
  2.9 64.3 %all_to_all.10 = f32[128,4,1024]{2,1,0:T(4,128)S(1)} all-to-all(f32[128,4,1024]{2,1,0:T(4,128)S(1)} %shard_map.50.sent_ref), channel_id=1, replica_groups=mesh['shift'=4,'far'=8,'near'=2,'core'=2,'tp'=2] {'far','core','near','tp'}, dimensions={0} | all-to-all | bytes 4194304 | tf_op jit(solution)/shard_map/all_to_all | solution.py:200
  67.3 4.0 %shard_map.51 = (f32[64,2,4,1024]{3,2,1,0:T(4,128)S(1)}, f32[128,4,1024]{2,1,0:T(4,128)}) custom-call(f32[64,2,4,1024]{3,2,1,0:T(4,128)S(1)} %bitcast.3, f32[128,4,1024]{2,1,0:T(4,128)S(1)} %shard_map.50.sent_ref), custom_call_target="tpu_custom_call" | custom-call | flops 2063597568 | bytes 4194304 | tf_op jit(solution)/shard_map/pallas_call | solution.py:115
  71.3 0.0 copy-start
  71.3 57.0 %all_to_all.11.back_ref = f32[128,4,1024]{2,1,0:T(4,128)S(1)} all-to-all(f32[128,4,1024]{2,1,0:T(4,128)S(1)} %bitcast.2), channel_id=1, replica_groups=mesh['shift'=4,'far'=8,'near'=2,'core'=2,'tp'=2] {'far','core','near','tp'}, dimensions={0} | all-to-all | bytes 4194304 | tf_op jit(solution)/shard_map/all_to_all | solution.py:203
  128.3 0.0 copy-done
  128.3 1.4 %shard_map.52 = f32[128,4,1024]{2,1,0:T(4,128)} custom-call(f32[128,4,1024]{2,1,0:T(4,128)S(1)} %copy-done, f32[128,4,1024]{2,1,0:T(4,128)S(1)} %all_to_all.11.back_ref), custom_call_target="tpu_custom_call" | custom-call | flops 524288 | bytes 2097152 | tf_op jit(solution)/shard_map/pallas_call | solution.py:182
Async XLA Ops:
  71.3 57.0 %copy-start = (f32[128,4,1024]{2,1,0:T(4,128)S(1)}, f32[128,4,1024]{2,1,0:T(4,128)}, u32[]{:S(2)}) copy-start(f32[128,4,1024]{2,1,0:T(4,128)} %weight_ref.1) | copy-start | bytes 6291460

commit v4 on v3

--- a/solution.py
+++ b/solution.py
@@ -8,8 +8,8 @@
 from jax.sharding import PartitionSpec as P
 
 ITERS = 3
-MOMENTUM_PIECES = 8
-WEIGHT_PIECES = 8
+MOMENTUM_PIECES = 4
+WEIGHT_PIECES = 4
 GROUP = ("far", "core", "near", "tp")
 
 
@@ -100,8 +100,10 @@
         parts.append(parts_of(whole_ref[mat]))
     steps = step_matrices([gram_of(*one) for one in parts])
     for mat, (step, (high, middle, low)) in enumerate(zip(steps, parts)):
-        right = (jnp.concatenate([high, middle], axis=0), jnp.concatenate([low, high], axis=0))
-        change = product_of(left_parts(step), right)
+        step_high, step_middle, _ = parts_of(step)
+        change = dot(step_high, middle, PLAIN) + dot(
+            jnp.concatenate([step_high, step_middle], axis=1), jnp.concatenate([high, high], axis=0), PLAIN
+        )
         for sender in range(senders):
             row, half = divmod(sender, halves)
             out_ref[sender, mat] = change[row * few : (row + 1) * few, half * wide : (half + 1) * wide]

time: 130 us -> 130 us (level)
  no operation moved by 1% of the time
where the time goes in v4:
time: 130 us; the launch traced here: 129 us
  blocking collectives  121 us (93%)
  Pallas kernels  7.43 us (6%)
    all_to_all x1, blocking collectives, body(): moved = lax.all_to_all(sent, GROUP, split_axis=0, concat_axis=0, tiled=True)  64.3 us
    all_to_all x1, blocking collectives, body(): lax.all_to_all(change.reshape(mats, few, wide), GROUP, split_axis=0, conc...  57 us
    pallas_call x1, Pallas kernels, update_matrices(): pl.pallas_call(functools.partial(matrices_kernel, halves), out_shape=[jax...  3.75 us

profile of v4, /device:TPU:1, one launch (start us, length us, event | category | flops | bytes accessed | tf_op | source)
XLA Modules:
  0.0 129.4 jit_solution(4083012978262180996)
XLA Ops:
  0.6 2.3 %shard_map.50.sent_ref = f32[128,4,1024]{2,1,0:T(4,128)S(1)} custom-call(f32[128,4,1024]{2,1,0:T(4,128)} %grad_ref.1, f32[128,4,1024]{2,1,0:T(4,128)} %moment_ref.1), custom_call_target="tpu_custom_call" | custom-call | flops 1048576 | bytes 4194304 | tf_op jit(solution)/shard_map/pallas_call | solution.py:150
  2.9 64.3 %all_to_all.10 = f32[128,4,1024]{2,1,0:T(4,128)S(1)} all-to-all(f32[128,4,1024]{2,1,0:T(4,128)S(1)} %shard_map.50.sent_ref), channel_id=1, replica_groups=mesh['shift'=4,'far'=8,'near'=2,'core'=2,'tp'=2] {'far','core','near','tp'}, dimensions={0} | all-to-all | bytes 4194304 | tf_op jit(solution)/shard_map/all_to_all | solution.py:202
  67.2 3.8 %shard_map.51 = (f32[64,2,4,1024]{3,2,1,0:T(4,128)S(1)}, f32[128,4,1024]{2,1,0:T(4,128)}) custom-call(f32[64,2,4,1024]{3,2,1,0:T(4,128)S(1)} %bitcast.3, f32[128,4,1024]{2,1,0:T(4,128)S(1)} %shard_map.50.sent_ref), custom_call_target="tpu_custom_call" | custom-call | flops 2063597568 | bytes 4194304 | tf_op jit(solution)/shard_map/pallas_call | solution.py:117
  71.0 0.0 copy-start
  71.0 57.0 %all_to_all.11.back_ref = f32[128,4,1024]{2,1,0:T(4,128)S(1)} all-to-all(f32[128,4,1024]{2,1,0:T(4,128)S(1)} %bitcast.2), channel_id=1, replica_groups=mesh['shift'=4,'far'=8,'near'=2,'core'=2,'tp'=2] {'far','core','near','tp'}, dimensions={0} | all-to-all | bytes 4194304 | tf_op jit(solution)/shard_map/all_to_all | solution.py:205
  128.0 0.0 copy-done
  128.0 1.4 %shard_map.52 = f32[128,4,1024]{2,1,0:T(4,128)} custom-call(f32[128,4,1024]{2,1,0:T(4,128)S(1)} %copy-done, f32[128,4,1024]{2,1,0:T(4,128)S(1)} %all_to_all.11.back_ref), custom_call_target="tpu_custom_call" | custom-call | flops 524288 | bytes 2097152 | tf_op jit(solution)/shard_map/pallas_call | solution.py:184
Async XLA Ops:
  71.0 57.0 %copy-start = (f32[128,4,1024]{2,1,0:T(4,128)S(1)}, f32[128,4,1024]{2,1,0:T(4,128)}, u32[]{:S(2)}) copy-start(f32[128,4,1024]{2,1,0:T(4,128)} %weight_ref.1) | copy-start | bytes 6291460

commit v5 on v3

--- a/solution.py
+++ b/solution.py
@@ -196,11 +196,14 @@
 def body(grad_stack, moment_stack, weight_stack):
     mats, few, wide = grad_stack.shape
     group, halves = lax.axis_size(GROUP), lax.axis_size(GROUP[-1])
+    far = lax.axis_size(GROUP[0])
+    plane = group // far
+    members = [[((z + far // 2) % far) * plane + one for z in range(far) for one in range(plane)]]
     sent = momentum_of(grad_stack, moment_stack)
-    moved = lax.all_to_all(sent, GROUP, split_axis=0, concat_axis=0, tiled=True)
+    moved = lax.all_to_all(sent, GROUP, split_axis=0, concat_axis=0, tiled=True, axis_index_groups=members)
     moved = moved.reshape(group, mats // group, few, wide)
     change, new_momentum = update_matrices(moved, sent, group // halves, halves)
-    back = lax.all_to_all(change.reshape(mats, few, wide), GROUP, split_axis=0, concat_axis=0, tiled=True)
+    back = lax.all_to_all(change.reshape(mats, few, wide), GROUP, split_axis=0, concat_axis=0, tiled=True, axis_index_groups=members)
     return (weights_of(weight_stack, back), new_momentum)
 
 

time: 130 us -> 128 us (0.985)
  blocking collectives: 121 us -> 119 us
    all_to_all x1, blocking collectives: 64.3 us -> 62.5 us  [body(): lax.all_to_all(sent, GROUP, split_axis=0, concat_axis=0, tiled=True, axis...]
where the time goes in v5:
time: 128 us
  blocking collectives  119 us (93%)
  Pallas kernels  7.76 us (6%)
    all_to_all x1, blocking collectives, body(): lax.all_to_all(sent, GROUP, split_axis=0, concat_axis=0, tiled=True, axis...  62.5 us
    all_to_all x1, blocking collectives, body(): lax.all_to_all(change.reshape(mats, few, wide), GROUP, split_axis=0, conc...  56.8 us
    pallas_call x1, Pallas kernels, update_matrices(): pl.pallas_call(functools.partial(matrices_kernel, halves), out_shape=[jax...  4.05 us

profile of v5, /device:TPU:1, one launch (start us, length us, event | category | flops | bytes accessed | tf_op | source)
XLA Modules:
  0.0 127.7 jit_solution(6195449170765154873)
XLA Ops:
  0.6 2.3 %shard_map.50.sent_ref = f32[128,4,1024]{2,1,0:T(4,128)S(1)} custom-call(f32[128,4,1024]{2,1,0:T(4,128)} %grad_ref.1, f32[128,4,1024]{2,1,0:T(4,128)} %moment_ref.1), custom_call_target="tpu_custom_call" | custom-call | flops 1048576 | bytes 4194304 | tf_op jit(solution)/shard_map/pallas_call | solution.py:148
  2.9 62.5 %all_to_all.10 = f32[128,4,1024]{2,1,0:T(4,128)S(1)} all-to-all(f32[128,4,1024]{2,1,0:T(4,128)S(1)} %shard_map.50.sent_ref), channel_id=1, replica_groups={{32,33,36,37,34,35,38,39,40,41,44,45,42,43,46,47,48,49,52,53,50,51,54,5..., dimensions={0} | all-to-all | bytes 4194304 | tf_op jit(solution)/shard_map/all_to_all | solution.py:203
  65.4 4.1 %shard_map.51 = (f32[64,2,4,1024]{3,2,1,0:T(4,128)S(1)}, f32[128,4,1024]{2,1,0:T(4,128)}) custom-call(f32[64,2,4,1024]{3,2,1,0:T(4,128)S(1)} %bitcast.3, f32[128,4,1024]{2,1,0:T(4,128)S(1)} %shard_map.50.sent_ref), custom_call_target="tpu_custom_call" | custom-call | flops 2063597568 | bytes 4194304 | tf_op jit(solution)/shard_map/pallas_call | solution.py:115
  69.5 0.0 copy-start
  69.5 56.8 %all_to_all.11.back_ref = f32[128,4,1024]{2,1,0:T(4,128)S(1)} all-to-all(f32[128,4,1024]{2,1,0:T(4,128)S(1)} %bitcast.2), channel_id=1, replica_groups={{32,33,36,37,34,35,38,39,40,41,44,45,42,43,46,47,48,49,52,53,50,51,54,5..., dimensions={0} | all-to-all | bytes 4194304 | tf_op jit(solution)/shard_map/all_to_all | solution.py:206
  126.3 0.0 copy-done
  126.3 1.4 %shard_map.52 = f32[128,4,1024]{2,1,0:T(4,128)} custom-call(f32[128,4,1024]{2,1,0:T(4,128)S(1)} %copy-done, f32[128,4,1024]{2,1,0:T(4,128)S(1)} %all_to_all.11.back_ref), custom_call_target="tpu_custom_call" | custom-call | flops 524288 | bytes 2097152 | tf_op jit(solution)/shard_map/pallas_call | solution.py:182
Async XLA Ops:
  69.5 56.8 %copy-start = (f32[128,4,1024]{2,1,0:T(4,128)S(1)}, f32[128,4,1024]{2,1,0:T(4,128)}, u32[]{:S(2)}) copy-start(f32[128,4,1024]{2,1,0:T(4,128)} %weight_ref.1) | copy-start | bytes 6291460

commit v6 on v5

--- a/solution.py
+++ b/solution.py
@@ -198,7 +198,7 @@
     group, halves = lax.axis_size(GROUP), lax.axis_size(GROUP[-1])
     far = lax.axis_size(GROUP[0])
     plane = group // far
-    members = [[((z + far // 2) % far) * plane + one for z in range(far) for one in range(plane)]]
+    members = [[((z + far // 2 - 1) % far) * plane + one for z in range(far) for one in range(plane)]]
     sent = momentum_of(grad_stack, moment_stack)
     moved = lax.all_to_all(sent, GROUP, split_axis=0, concat_axis=0, tiled=True, axis_index_groups=members)
     moved = moved.reshape(group, mats // group, few, wide)

time: 128 us -> 131 us (1.023)
  blocking collectives: 119 us -> 123 us
    all_to_all x1, blocking collectives: 62.5 us -> 65.4 us  [body(): lax.all_to_all(sent, GROUP, split_axis=0, concat_axis=0, tiled=True, axis...]
where the time goes in v6:
time: 131 us
  blocking collectives  123 us (94%)
  Pallas kernels  7.76 us (6%)
    all_to_all x1, blocking collectives, body(): lax.all_to_all(sent, GROUP, split_axis=0, concat_axis=0, tiled=True, axis...  65.4 us
    all_to_all x1, blocking collectives, body(): lax.all_to_all(change.reshape(mats, few, wide), GROUP, split_axis=0, conc...  57.3 us
    pallas_call x1, Pallas kernels, update_matrices(): pl.pallas_call(functools.partial(matrices_kernel, halves), out_shape=[jax...  4.05 us

profile of v6, /device:TPU:1, one launch (start us, length us, event | category | flops | bytes accessed | tf_op | source)
XLA Modules:
  0.0 131.1 jit_solution(18353380733802063771)
XLA Ops:
  0.6 2.3 %shard_map.50.sent_ref = f32[128,4,1024]{2,1,0:T(4,128)S(1)} custom-call(f32[128,4,1024]{2,1,0:T(4,128)} %grad_ref.1, f32[128,4,1024]{2,1,0:T(4,128)} %moment_ref.1), custom_call_target="tpu_custom_call" | custom-call | flops 1048576 | bytes 4194304 | tf_op jit(solution)/shard_map/pallas_call | solution.py:148
  2.9 65.4 %all_to_all.10 = f32[128,4,1024]{2,1,0:T(4,128)S(1)} all-to-all(f32[128,4,1024]{2,1,0:T(4,128)S(1)} %shard_map.50.sent_ref), channel_id=1, replica_groups={{24,25,28,29,26,27,30,31,32,33,36,37,34,35,38,39,40,41,44,45,42,43,46,4..., dimensions={0} | all-to-all | bytes 4194304 | tf_op jit(solution)/shard_map/all_to_all | solution.py:203
  68.3 4.0 %shard_map.51 = (f32[64,2,4,1024]{3,2,1,0:T(4,128)S(1)}, f32[128,4,1024]{2,1,0:T(4,128)}) custom-call(f32[64,2,4,1024]{3,2,1,0:T(4,128)S(1)} %bitcast.3, f32[128,4,1024]{2,1,0:T(4,128)S(1)} %shard_map.50.sent_ref), custom_call_target="tpu_custom_call" | custom-call | flops 2063597568 | bytes 4194304 | tf_op jit(solution)/shard_map/pallas_call | solution.py:115
  72.4 0.0 copy-start
  72.4 57.3 %all_to_all.11.back_ref = f32[128,4,1024]{2,1,0:T(4,128)S(1)} all-to-all(f32[128,4,1024]{2,1,0:T(4,128)S(1)} %bitcast.2), channel_id=1, replica_groups={{24,25,28,29,26,27,30,31,32,33,36,37,34,35,38,39,40,41,44,45,42,43,46,4..., dimensions={0} | all-to-all | bytes 4194304 | tf_op jit(solution)/shard_map/all_to_all | solution.py:206
  129.7 0.0 copy-done
  129.7 1.4 %shard_map.52 = f32[128,4,1024]{2,1,0:T(4,128)} custom-call(f32[128,4,1024]{2,1,0:T(4,128)S(1)} %copy-done, f32[128,4,1024]{2,1,0:T(4,128)S(1)} %all_to_all.11.back_ref), custom_call_target="tpu_custom_call" | custom-call | flops 524288 | bytes 2097152 | tf_op jit(solution)/shard_map/pallas_call | solution.py:182
Async XLA Ops:
  72.4 57.3 %copy-start = (f32[128,4,1024]{2,1,0:T(4,128)S(1)}, f32[128,4,1024]{2,1,0:T(4,128)}, u32[]{:S(2)}) copy-start(f32[128,4,1024]{2,1,0:T(4,128)} %weight_ref.1) | copy-start | bytes 6291460
